TPU v7x, 32 devices: a whole 2x2x4 slice. The times are simulated.
32 devices in a mesh: ka: 4 (over y, x), ga: 8 (over z, core).
Axes of the slice: x: 2, y: 2, z: 4, core: 2. Of those that a mesh axis runs over, the one named last changes fastest.
Arguments:
- coeffs: bfloat16 [4, 1, 65536, 2, 512], P('ka', None, 'ga'), may hold values from -0.5 to 0.5
- counts: int32 [4, 1], replicated, may hold values from 32768 to 65536
- block_map: int32 [4, 1, 2048], replicated, may hold values from 0 to 2047, as said below
- wrap: int32 [4, 1, 2048], replicated, may hold values from 0 to 31
Outputs:
- margins: float32 [4, 512, 1, 2, 512], P('ka', 'ga')
Inputs may be any that keep to these rules, and one draw needn't show every extreme that they name: For each k-point and line, block_map is a permutation of the 2048 blocks. Counting G-shards as runs of 256 blocks, at most 33 blocks of one shard have their partner blocks in any one shard, and for each k-point and line some pair of shards reaches 33.
All inputs are finite; a program needn't handle non-finite values.
Results may differ from a plain program's by a relative error of at most 0.0003.
Values may be sent and summed in bfloat16 or wider, within the bound.
No kernel may reach another device: no remote copies, remote signals or barrier semaphores. Data moves between devices by JAX's collectives and lax.ppermute only.
A program may use at most 128 MiB of HBM per device.

v0:
```python
import jax
import jax.numpy as jnp
from jax import lax
from jax.sharding import PartitionSpec as P

BLK = 32


def from_behind(value, axis, steps):
    count = lax.axis_size(axis)
    pairs = [(source, (source + steps) % count) for source in range(count)]
    return lax.ppermute(value, axis, pairs)


def slot_table(dest, ranking, values, shard_count, capacity):
    shard_ids = jnp.arange(shard_count, dtype=jnp.int32)
    slot_ids = jnp.arange(capacity, dtype=jnp.int32)
    hit = (dest[:, :, None, None] == shard_ids[None, None, :, None]) & (
        ranking[:, :, None, None] == slot_ids[None, None, None, :]
    )
    return jnp.sum(jnp.where(hit, values[:, :, None, None], 0), axis=1)


def pick_rows(source, picks):
    return jax.vmap(lambda rows_in, index_in: jnp.take(rows_in, index_in, axis=0))(source, picks)


def local(coeffs, counts, block_map, wrap):
    held_k = coeffs[0]
    line_count, g_rows, _, band_count = held_k.shape
    shard_count = lax.axis_size("ga")
    per_shard = g_rows // BLK
    block_total = block_map.shape[-1]
    capacity = block_total // (shard_count * shard_count) + 1
    k_index = lax.axis_index("ka")
    g_index = lax.axis_index("ga")
    k_total = counts.shape[0]
    count_here = counts[k_index]
    count_next = counts[(k_index + 1) % k_total]
    block_src = block_map[k_index]
    wrap_src = wrap[k_index]
    lane_ids = jnp.arange(BLK, dtype=jnp.int32)
    block_mine = lax.dynamic_slice_in_dim(block_src, g_index * per_shard, per_shard, 1)
    wrap_mine = lax.dynamic_slice_in_dim(wrap_src, g_index * per_shard, per_shard, 1)
    lane_shift = (lane_ids[None, None, :] + wrap_mine[:, :, None]) % BLK
    src_rows = block_mine[:, :, None] * BLK + lane_shift
    own_rows = g_index * g_rows + jnp.arange(g_rows, dtype=jnp.int32).reshape(per_shard, BLK)
    usable = (own_rows[None] < count_here[:, None, None]) & (src_rows < count_next[:, None, None])
    usable = usable.reshape(line_count, g_rows)
    masked_k = jnp.where(usable[:, :, None, None], held_k, jnp.zeros((), held_k.dtype))
    source_dev = block_mine // per_shard
    same_dev = source_dev[:, :, None] == source_dev[:, None, :]
    earlier = jnp.arange(per_shard)[:, None] > jnp.arange(per_shard)[None, :]
    rank_mine = jnp.sum((same_dev & earlier[None]).astype(jnp.int32), axis=2)
    coming = from_behind(held_k, "ka", -1)
    blocks_held = masked_k.reshape(line_count, per_shard, BLK, 2, band_count)
    back_lanes = (lane_ids[None, None, :] - wrap_mine[:, :, None]) % BLK
    rotated = jax.vmap(jax.vmap(lambda rows_in, index_in: jnp.take(rows_in, index_in, axis=0)))(
        blocks_held, back_lanes
    )
    local_ids = jnp.arange(per_shard, dtype=jnp.int32)[None, :]
    send_table = slot_table(source_dev, rank_mine, local_ids, shard_count, capacity)
    outgoing = pick_rows(rotated, send_table.reshape(line_count, -1))
    outgoing = outgoing.reshape(line_count, shard_count, capacity * BLK, 2, band_count)
    incoming = lax.all_to_all(outgoing, "ga", split_axis=1, concat_axis=1, tiled=True)
    incoming = incoming.reshape(line_count, shard_count * capacity * BLK, 2, band_count)
    inverse = jax.vmap(
        lambda perm_in: jnp.zeros((block_total,), jnp.int32)
        .at[perm_in]
        .set(jnp.arange(block_total, dtype=jnp.int32))
    )(block_src)
    target_mine = lax.dynamic_slice_in_dim(inverse, g_index * per_shard, per_shard, 1)
    sender = target_mine // per_shard
    to_me = block_src // per_shard == g_index
    rank_to_me = (
        jnp.cumsum(to_me.reshape(line_count, shard_count, per_shard).astype(jnp.int32), axis=2) - 1
    ).reshape(line_count, block_total)
    rank_sent = jnp.take_along_axis(rank_to_me, target_mine, axis=1)
    row_index = (
        (sender * capacity + rank_sent)[:, :, None] * BLK + lane_ids[None, None, :]
    ).reshape(line_count, g_rows)
    left_side = pick_rows(incoming, row_index)
    rows_here = band_count // shard_count
    products = jnp.einsum("lgcm,lgdn->mlcdn", left_side, coming, preferred_element_type=jnp.float32)
    real_part = products[:, :, 0, 0] + products[:, :, 1, 1]
    imag_part = products[:, :, 0, 1] - products[:, :, 1, 0]
    summed = lax.psum(jnp.stack([real_part, imag_part], axis=2), "ga")
    result = lax.dynamic_slice_in_dim(summed, g_index * rows_here, rows_here, 0)
    return result[None]


def solution(mesh):
    placed = (P("ka", None, "ga", None, None), P(), P(), P())
    return jax.shard_map(
        local,
        mesh=mesh,
        in_specs=placed,
        out_specs=P("ka", "ga", None, None, None),
        check_vma=False,
    )
```

profile of v0, /device:TPU:0, one launch (start us, length us, event | category | flops | bytes accessed | tf_op | source)
XLA Modules:
  0.0 826.9 jit_solution(5665315744447065316)
XLA Ops:
  6.5 0.8 and_select_fusion
  7.3 0.2 convert_reduce_fusion
  7.5 0.7 select_reduce_fusion
  8.6 0.1 broadcast_in_dim.90
  8.7 0.1 broadcast_in_dim.91
  9.0 1.4 constant_dynamic-slice_fusion.1
  10.4 1.6 compare_and_fusion
  12.0 21.3 %broadcast_select_fusion.2 = bf16[1,256,32,2,512]{4,3,2,1,0:T(2,128)(2,1)} fusion(bf16[1,256,32,2,512]{4,3,2,1,0:T(2,128)(2,1)} %bitcast.68, pred[256,32]{1,0:T(8,128)(4,1)S(1)} %get-tuple-element.14), kind=kLoop, calls=%fused_computation.7 | loop fusion | flops 8388608 | bytes 33562624 | tf_op jit(solution)/shard_map/jit(_where)/select_n | solution.py:50
  33.4 99.0 %gather_fusion.1 = bf16[8192,2,512]{2,1,0:T(2,128)(2,1)} fusion(bf16[1,256,32,2,512]{4,3,2,1,0:T(2,128)(2,1)} %broadcast_select_fusion.2, s32[8192]{0:T(1024)S(1)} %reshape.1065), kind=kCustom, calls=%fused_computation.1 | custom fusion | bytes 33652736 | tf_op jit(solution)/shard_map/vmap(vmap(jit(_take)))/gather | solution.py:58
  132.4 21.7 %broadcast_select_fusion.3 = bf16[1,256,32,2,512]{4,3,2,1,0:T(2,128)(2,1)} fusion(bf16[1,256,32,2,512]{4,3,2,1,0:T(2,128)(2,1)} %bitcast.69, pred[256,32]{1,0:T(8,128)(4,1)S(1)} %get-tuple-element.13), kind=kLoop, calls=%fused_computation.8 | loop fusion | flops 8388608 | bytes 33562624 | tf_op jit(solution)/shard_map/vmap(vmap(jit(_take)))/select_n | solution.py:58
  154.0 47.2 %gather_fusion.2 = bf16[264,32,2,512]{3,2,1,0:T(2,128)(2,1)} fusion(bf16[1,256,32,2,512]{4,3,2,1,0:T(2,128)(2,1)} %broadcast_select_fusion.3, s32[264]{0:T(512)S(1)} %fusion.45), kind=kCustom, calls=%fused_computation.2 | custom fusion | bytes 34605120 | tf_op jit(solution)/shard_map/vmap(jit(_take))/gather | solution.py:25
  201.2 25.0 %broadcast_select_fusion = bf16[1,8,1056,2,512]{4,3,2,0,1:T(2,128)(2,1)} fusion(bf16[1,8,1056,2,512]{4,3,2,0,1:T(2,128)(2,1)} %bitcast.67, pred[8,1056]{1,0:T(8,128)(4,1)S(1)} %broadcast_in_dim.91), kind=kLoop, calls=%fused_computation.5 | loop fusion | flops 8650752 | bytes 34611456 | tf_op jit(solution)/shard_map/vmap(jit(_take))/select_n | solution.py:25
  226.2 6.4 all-to-all-start
  232.7 15.8 %copy.58 = bf16[1,1,8192,2,512]{4,2,3,1,0:T(8,128)(2,1)} copy(bf16[1,1,8192,2,512]{4,3,2,1,0:T(2,128)(2,1)} %param.4) | data formatting | bytes 33554432 | tf_op args[0]
  248.5 3.4 collective-permute-start
  251.8 0.7 compare_select_fusion.5
  252.6 0.6 reduce-window.6
  253.2 0.2 slice_reduce_fusion
  253.5 0.1 and_reduce_fusion
  253.7 8.2 scatter_custom_fusion
  262.2 1.7 gather_fusion
  264.0 0.1 add.375
  264.3 0.1 add.377
  264.7 343.0 %all-to-all-done = bf16[1,8,1056,2,512]{4,3,2,0,1:T(2,128)(2,1)} async-done(((bf16[1,8,1056,2,512]{4,3,2,0,1:T(2,128)(2,1)}), bf16[1,8,1056,2,512]{4,3,2,0,1:T(2,128)(2,1)}, u32[]{:S(2)}, u32[]{:S(2)}) %all-to-all-start) | async-done | bytes 17301536 | tf_op jit(solution)/shard_map/all_to_all | solution.py:65
  607.7 91.4 %gather_fusion.3 = bf16[8192,2,512]{2,1,0:T(2,128)(2,1)} fusion(bf16[1,8448,2,512]{3,2,1,0:T(2,128)(2,1)} %bitcast.20, s32[8192]{0:T(1024)S(1)} %bitcast.65), kind=kCustom, calls=%fused_computation.3 | custom fusion | bytes 33619968 | tf_op jit(solution)/shard_map/vmap(jit(_take))/gather | solution.py:25
  699.2 31.5 %fusion.3 = bf16[8192,2,512,1]{2,1,0,3:T(2,128)(2,1)S(1)} fusion(bf16[8192,2,512]{2,1,0:T(2,128)(2,1)} %gather_fusion.3, pred[8192]{0:T(1024)(128)(4,1)S(1)} %compare_and_fusion.1), kind=kLoop, calls=%fused_computation.13 | loop fusion | flops 8388608 | bytes 33562624 | tf_op jit(solution)/shard_map/vmap(jit(_take))/select_n | solution.py:25
  730.7 20.7 %fusion.4 = f32[512,1,2,2,512]{4,0,3,2,1:T(8,128)S(1)} fusion(bf16[1,8192,2,512]{3,1,2,0:T(8,128)(2,1)} %collective-permute-done, bf16[8192,2,512,1]{2,1,0,3:T(2,128)(2,1)S(1)} %fusion.3), kind=kOutput, calls=%fused_computation.14 | convolution fusion | flops 17179869184 | bytes 37748736 | tf_op jit(solution)/shard_map/lgcm,lgdn->mlcdn/dot_general | solution.py:84
  751.4 0.5 fusion.10
  751.9 1.5 pad_maximum_fusion
  753.4 64.8 %all-reduce.2.cloned.1.call-done = f32[512,1,2,512]{3,0,2,1:T(8,128)} async-done(((f32[512,1,2,512]{3,0,2,1:T(8,128)}), f32[512,1,2,512]{3,0,2,1:T(8,128)}) %all-reduce.2.cloned.1.call-update) | async-done | bytes 2097168 | tf_op jit(solution)/shard_map/psum | solution.py:87
  818.2 1.0 dynamic-slice_bitcast_fusion
  819.1 0.9 copy.48
  (47 shorter events, 1.6 us)
Async XLA Ops:
  226.2 381.5 %all-to-all-start = ((bf16[1,8,1056,2,512]{4,3,2,0,1:T(2,128)(2,1)}), bf16[1,8,1056,2,512]{4,3,2,0,1:T(2,128)(2,1)}, u32[]{:S(2)}, u32[]{:S(2)}) async-start(bf16[1,8,1056,2,512]{4,3,2,0,1:T(2,128)(2,1)} %broadcast_select_fusion), calls=%async_computation | async-start | bytes 34603008 | tf_op jit(solution)/shard_map/all_to_all | solution.py:65
  232.6 20.8 %copy-start = (s32[2]{0:T(128)S(1)}, s32[2]{0:T(128)}, u32[]{:S(2)}) copy-start(s32[2]{0:T(128)} %constant.184) | copy-start | bytes 28
  232.6 20.9 %copy-start.1 = (s32[2]{0:T(128)S(1)}, s32[2]{0:T(128)}, u32[]{:S(2)}) copy-start(s32[2]{0:T(128)} %constant.187) | copy-start | bytes 28
  232.6 585.6 %all-reduce.2.cloned.1.call-start = ((), (), s32[]{:S(2)}) async-start(), calls=%async_computation.1 | async-start | bytes 4194304 | tf_op jit(solution)/shard_map/psum | solution.py:87
  248.5 482.2 %collective-permute-start = (bf16[1,8192,2,512]{3,1,2,0:T(8,128)(2,1)}, bf16[1,8192,2,512]{3,1,2,0:T(8,128)(2,1)}, u32[]{:S(2)}, u32[]{:S(2)}) collective-permute-start(bf16[1,8192,2,512]{3,1,2,0:T(8,128)(2,1)} %bitcast.63), channel_id=1, source_target_pairs={{0,24},{8,0},{16,8},{24,16},{1,25},{9,1},{17,9},{25,17},{2,26},{10... | collective-permute-start | bytes 50331656 | tf_op jit(solution)/shard_map/ppermute | solution.py:12
Sparse Core Ops, SparseCore 0:
  753.5 64.6 all-reduce.1
where the time goes:
time: 827 us
  waiting for transfers between devices  408 us (49%)
  local copies, waits for them, and re-layouts  268 us (32%)
  other arithmetic  107 us (13%)
  matrix products  20.7 us (3%)
  between operations  13.7 us (2%)
  starting transfers between devices  9.76 us (1%)
    all_to_all x1, waiting for transfers between devices, local(): lax.all_to_all(outgoing, 'ga', split_axis=1, concat_axis=1, tiled=True)  343 us
    gather x4, local copies, waits for them, and re-layouts, pick_rows(): jnp.take(rows_in, index_in, axis=0)  139 us
    gather x3, local copies, waits for them, and re-layouts, local(): jnp.take(rows_in, index_in, axis=0)  99.2 us
    psum x1, waiting for transfers between devices, local(): summed = lax.psum(jnp.stack([real_part, imag_part], axis=2), 'ga')  64.8 us
    select_n x4, other arithmetic, pick_rows(): jnp.take(rows_in, index_in, axis=0)  56.6 us
    unnamed x9, local copies, waits for them, and re-layouts  24.2 us
    select_n x2, other arithmetic, local(): jnp.take(rows_in, index_in, axis=0)  21.7 us
    select_n x1, other arithmetic, local(): jnp.where(usable[:, :, None, None], held_k, jnp.zeros((), held_k.dtype))  21.3 us
  transfers between devices with their start and end apart: 3, of which 2 were waited for; matrix products, arithmetic and copies ran while one was open for 18% of the time, Pallas kernels for 0%

commit v1 on v0

--- a/solution.py
+++ b/solution.py
@@ -1,9 +1,18 @@
+import functools
 import jax
 import jax.numpy as jnp
 from jax import lax
 from jax.sharding import PartitionSpec as P
 
 BLK = 32
+
+
+def _number_stocks(s0, named_axis):
+    d_next = lax.all_gather(s0, named_axis)
+    return jnp.sum(d_next, axis=0)
+
+
+answer_spots = functools.partial(_number_stocks, named_axis="ga")
 
 
 def from_behind(value, axis, steps):
@@ -84,7 +93,7 @@
     products = jnp.einsum("lgcm,lgdn->mlcdn", left_side, coming, preferred_element_type=jnp.float32)
     real_part = products[:, :, 0, 0] + products[:, :, 1, 1]
     imag_part = products[:, :, 0, 1] - products[:, :, 1, 0]
-    summed = lax.psum(jnp.stack([real_part, imag_part], axis=2), "ga")
+    summed = answer_spots(jnp.stack([real_part, imag_part], axis=2))
     result = lax.dynamic_slice_in_dim(summed, g_index * rows_here, rows_here, 0)
     return result[None]
 

time: 827 us -> 921 us (1.11)
  waiting for transfers between devices: 408 us -> 494 us
    all_gather x0 -> x1, waiting for transfers between devices: none -> 151 us  [_number_stocks(): d_next = lax.all_gather(s0, named_axis)]
    psum x1 -> x0, waiting for transfers between devices: 64.8 us -> none  [local(): summed = lax.psum(jnp.stack([real_part, imag_part], axis=2), 'ga')]
  transfers between devices with their start and end apart: 3 -> 3, of which waited for: 2 -> 2; matrix products, arithmetic and copies ran while one was open for 18% -> 16% of each run, Pallas kernels for 0% -> 0%
where the time goes in v1:
time: 921 us; the launch traced here: 920 us
  waiting for transfers between devices  494 us (54%)
  local copies, waits for them, and re-layouts  267 us (29%)
  other arithmetic  115 us (12%)
  matrix products  20.7 us (2%)
  between operations  13.7 us (1%)
  starting transfers between devices  9.76 us (1%)
    all_to_all x1, waiting for transfers between devices, local(): lax.all_to_all(outgoing, 'ga', split_axis=1, concat_axis=1, tiled=True)  343 us
    all_gather x1, waiting for transfers between devices, _number_stocks(): d_next = lax.all_gather(s0, named_axis)  151 us
    gather x4, local copies, waits for them, and re-layouts, pick_rows(): jnp.take(rows_in, index_in, axis=0)  139 us
    gather x3, local copies, waits for them, and re-layouts, local(): jnp.take(rows_in, index_in, axis=0)  99.2 us
    select_n x4, other arithmetic, pick_rows(): jnp.take(rows_in, index_in, axis=0)  56.6 us
    unnamed x9, local copies, waits for them, and re-layouts  24.2 us
    select_n x2, other arithmetic, local(): jnp.take(rows_in, index_in, axis=0)  21.7 us
    select_n x1, other arithmetic, local(): jnp.where(usable[:, :, None, None], held_k, jnp.zeros((), held_k.dtype))  21.3 us
  transfers between devices with their start and end apart: 3, of which 2 were waited for; matrix products, arithmetic and copies ran while one was open for 16% of the time, Pallas kernels for 0%

profile of v1, /device:TPU:0, one launch (start us, length us, event | category | flops | bytes accessed | tf_op | source)
XLA Modules:
  0.0 920.1 jit_solution(1610816842435526989)
XLA Ops:
  6.5 0.8 and_select_fusion
  7.3 0.2 convert_reduce_fusion
  7.5 0.7 select_reduce_fusion
  8.6 0.1 broadcast_in_dim.90
  8.7 0.1 broadcast_in_dim.91
  9.0 1.4 constant_dynamic-slice_fusion.1
  10.4 1.6 compare_and_fusion
  12.0 21.3 %broadcast_select_fusion.2 = bf16[1,256,32,2,512]{4,3,2,1,0:T(2,128)(2,1)} fusion(bf16[1,256,32,2,512]{4,3,2,1,0:T(2,128)(2,1)} %bitcast.69, pred[256,32]{1,0:T(8,128)(4,1)S(1)} %get-tuple-element.14), kind=kLoop, calls=%fused_computation.7 | loop fusion | flops 8388608 | bytes 33562624 | tf_op jit(solution)/shard_map/jit(_where)/select_n | solution.py:59
  33.4 99.0 %gather_fusion.1 = bf16[8192,2,512]{2,1,0:T(2,128)(2,1)} fusion(bf16[1,256,32,2,512]{4,3,2,1,0:T(2,128)(2,1)} %broadcast_select_fusion.2, s32[8192]{0:T(1024)S(1)} %reshape.1068), kind=kCustom, calls=%fused_computation.1 | custom fusion | bytes 33652736 | tf_op jit(solution)/shard_map/vmap(vmap(jit(_take)))/gather | solution.py:67
  132.4 21.7 %broadcast_select_fusion.3 = bf16[1,256,32,2,512]{4,3,2,1,0:T(2,128)(2,1)} fusion(bf16[1,256,32,2,512]{4,3,2,1,0:T(2,128)(2,1)} %bitcast.70, pred[256,32]{1,0:T(8,128)(4,1)S(1)} %get-tuple-element.13), kind=kLoop, calls=%fused_computation.8 | loop fusion | flops 8388608 | bytes 33562624 | tf_op jit(solution)/shard_map/vmap(vmap(jit(_take)))/select_n | solution.py:67
  154.0 47.2 %gather_fusion.2 = bf16[264,32,2,512]{3,2,1,0:T(2,128)(2,1)} fusion(bf16[1,256,32,2,512]{4,3,2,1,0:T(2,128)(2,1)} %broadcast_select_fusion.3, s32[264]{0:T(512)S(1)} %fusion.45), kind=kCustom, calls=%fused_computation.2 | custom fusion | bytes 34605120 | tf_op jit(solution)/shard_map/vmap(jit(_take))/gather | solution.py:34
  201.2 25.0 %broadcast_select_fusion = bf16[1,8,1056,2,512]{4,3,2,0,1:T(2,128)(2,1)} fusion(bf16[1,8,1056,2,512]{4,3,2,0,1:T(2,128)(2,1)} %bitcast.68, pred[8,1056]{1,0:T(8,128)(4,1)S(1)} %broadcast_in_dim.91), kind=kLoop, calls=%fused_computation.5 | loop fusion | flops 8650752 | bytes 34611456 | tf_op jit(solution)/shard_map/vmap(jit(_take))/select_n | solution.py:34
  226.2 6.4 all-to-all-start
  232.7 15.8 %copy.63 = bf16[1,1,8192,2,512]{4,2,3,1,0:T(8,128)(2,1)} copy(bf16[1,1,8192,2,512]{4,3,2,1,0:T(2,128)(2,1)} %param.4) | data formatting | bytes 33554432 | tf_op args[0]
  248.5 3.4 collective-permute-start
  251.8 0.7 compare_select_fusion.5
  252.6 0.6 reduce-window.6
  253.2 0.2 slice_reduce_fusion
  253.5 0.1 and_reduce_fusion
  253.7 8.2 scatter_custom_fusion
  262.2 1.7 gather_fusion
  264.0 0.1 add.373
  264.3 0.1 add.375
  264.7 343.0 %all-to-all-done = bf16[1,8,1056,2,512]{4,3,2,0,1:T(2,128)(2,1)} async-done(((bf16[1,8,1056,2,512]{4,3,2,0,1:T(2,128)(2,1)}), bf16[1,8,1056,2,512]{4,3,2,0,1:T(2,128)(2,1)}, u32[]{:S(2)}, u32[]{:S(2)}) %all-to-all-start) | async-done | bytes 17301536 | tf_op jit(solution)/shard_map/all_to_all | solution.py:74
  607.7 91.4 %gather_fusion.3 = bf16[8192,2,512]{2,1,0:T(2,128)(2,1)} fusion(bf16[1,8448,2,512]{3,2,1,0:T(2,128)(2,1)} %bitcast.20, s32[8192]{0:T(1024)S(1)} %bitcast.66), kind=kCustom, calls=%fused_computation.3 | custom fusion | bytes 33619968 | tf_op jit(solution)/shard_map/vmap(jit(_take))/gather | solution.py:34
  699.2 31.5 %fusion.3 = bf16[8192,2,512,1]{2,1,0,3:T(2,128)(2,1)S(1)} fusion(bf16[8192,2,512]{2,1,0:T(2,128)(2,1)} %gather_fusion.3, pred[8192]{0:T(1024)(128)(4,1)S(1)} %compare_and_fusion.1), kind=kLoop, calls=%fused_computation.13 | loop fusion | flops 8388608 | bytes 33562624 | tf_op jit(solution)/shard_map/vmap(jit(_take))/select_n | solution.py:34
  730.7 20.7 %fusion.4 = f32[512,1,2,2,512]{4,0,3,2,1:T(8,128)S(1)} fusion(bf16[1,8192,2,512]{3,1,2,0:T(8,128)(2,1)} %collective-permute-done, bf16[8192,2,512,1]{2,1,0,3:T(2,128)(2,1)S(1)} %fusion.3), kind=kOutput, calls=%fused_computation.14 | convolution fusion | flops 17179869184 | bytes 37748736 | tf_op jit(solution)/shard_map/lgcm,lgdn->mlcdn/dot_general | solution.py:93
  751.4 0.5 fusion.10
  751.9 1.5 pad_maximum_fusion
  753.4 150.8 %all-gather.3.cloned.1.call-done = f32[4096,1,2,512]{3,0,2,1:T(8,128)} async-done(((f32[512,1,2,512]{3,0,2,1:T(8,128)}), f32[4096,1,2,512]{3,0,2,1:T(8,128)}) %all-gather.3.cloned.1.call-update) | async-done | bytes 16777232 | tf_op jit(solution)/shard_map/all_gather | solution.py:11
  904.2 8.1 reduce.7
  912.3 0.9 copy.53
  (48 shorter events, 1.6 us)
Async XLA Ops:
  226.2 381.5 %all-to-all-start = ((bf16[1,8,1056,2,512]{4,3,2,0,1:T(2,128)(2,1)}), bf16[1,8,1056,2,512]{4,3,2,0,1:T(2,128)(2,1)}, u32[]{:S(2)}, u32[]{:S(2)}) async-start(bf16[1,8,1056,2,512]{4,3,2,0,1:T(2,128)(2,1)} %broadcast_select_fusion), calls=%async_computation | async-start | bytes 34603008 | tf_op jit(solution)/shard_map/all_to_all | solution.py:74
  232.6 20.8 %copy-start = (s32[2]{0:T(128)S(1)}, s32[2]{0:T(128)}, u32[]{:S(2)}) copy-start(s32[2]{0:T(128)} %constant.186) | copy-start | bytes 28
  232.6 20.9 %copy-start.1 = (s32[2]{0:T(128)S(1)}, s32[2]{0:T(128)}, u32[]{:S(2)}) copy-start(s32[2]{0:T(128)} %constant.189) | copy-start | bytes 28
  232.6 671.6 %all-gather.3.cloned.1.call-start = ((), (), s32[]{:S(2)}) async-start(), calls=%async_computation.1 | async-start | bytes 18874368 | tf_op jit(solution)/shard_map/all_gather | solution.py:11
  248.5 482.2 %collective-permute-start = (bf16[1,8192,2,512]{3,1,2,0:T(8,128)(2,1)}, bf16[1,8192,2,512]{3,1,2,0:T(8,128)(2,1)}, u32[]{:S(2)}, u32[]{:S(2)}) collective-permute-start(bf16[1,8192,2,512]{3,1,2,0:T(8,128)(2,1)} %bitcast.64), channel_id=1, source_target_pairs={{0,24},{8,0},{16,8},{24,16},{1,25},{9,1},{17,9},{25,17},{2,26},{10... | collective-permute-start | bytes 50331656 | tf_op jit(solution)/shard_map/ppermute | solution.py:21
Sparse Core Ops, SparseCore 0:
  753.6 150.6 all-gather.2
